TPU v7x, 32 devices: a whole 2x2x4 slice. The times are simulated.
32 devices in a mesh: dp: 2 (over x), tp: 16 (over z, y, core).
Axes of the slice: x: 2, y: 2, z: 4, core: 2. Of those that a mesh axis runs over, the one named last changes fastest.
Arguments:
- token_ids: int32 [2, 2048], P('dp'), parts along dimension 0
- route_idx: int32 [2, 2048, 8], P('dp'), parts along dimension 0
- embed_table: bfloat16 [50304, 2048], P('tp')
- attn_norm: bfloat16 [2048], replicated
- w_query: bfloat16 [2048, 2048], P(None, 'tp')
- w_key: bfloat16 [2048, 2048], P(None, 'tp')
- w_value: bfloat16 [2048, 2048], P(None, 'tp')
- w_out: bfloat16 [2048, 2048], P('tp')
- q_gain: bfloat16 [2048], P('tp')
- k_gain: bfloat16 [2048], P('tp')
- mlp_norm: bfloat16 [2048], replicated
- w_router: bfloat16 [2048, 64], replicated
- w_gate: bfloat16 [64, 2048, 1024], P(None, None, 'tp')
- w_up: bfloat16 [64, 2048, 1024], P(None, None, 'tp')
- w_down: bfloat16 [64, 1024, 2048], P(None, 'tp')
Outputs:
- output: bfloat16 [2, 2048, 2048], P('dp', 'tp'), parts along dimension 0
There are 2 independent parts. A program takes and returns all parts, laid end to end along the dimension named above; an argument that names none is the same for every part.
All inputs are finite; a program needn't handle non-finite values.
Results may differ from a plain program's by a relative error of at most 0.010359.
Values are sent between devices in bfloat16 or wider.
A program may use at most 1 GiB of HBM per device.

v0:
```python
import functools

import jax
import jax.numpy as jnp
from jax import lax
from jax.experimental import pallas as pl
from jax.experimental.pallas import tpu as pltpu
from jax.sharding import PartitionSpec as P

HEAD_DIM = 128
NORM_EPS = 1e-5
N_CHUNKS = 4
EXP_PER_STEP = 8
VMEM_LIMIT = 63 * 1024 * 1024


def rope_tables(seq_len):
    half_dim = HEAD_DIM // 2
    inv_freq = 1.0 / (10000.0 ** (jnp.arange(half_dim, dtype=jnp.float32) * (2.0 / HEAD_DIM)))
    angles = jnp.arange(seq_len, dtype=jnp.float32)[:, None] * inv_freq[None, :]
    return jnp.cos(angles), jnp.sin(angles)


N_STAGES = 6
N_Z, N_Y = 4, 2
GATHER_LAST = 8
MESH = pl.DeviceIdType.MESH


class Place:
    def __init__(self):
        self.me = lax.axis_index("tp")
        self.z = self.me // 4
        self.y = self.me % 4 // 2
        self.c = self.me % 2
        self.core_peer = self.me + 1 - 2 * self.c
        self.y_peer = self.me + 2 - 4 * self.y
        self.up = self.me + 4
        self.down = self.me - 4

    def index(self, zz, yy, cc):
        return zz * 4 + yy * 2 + cc


def remote(src, dst, send_sem, recv_sem, device):
    return pltpu.make_async_remote_copy(src_ref=src, dst_ref=dst, send_sem=send_sem, recv_sem=recv_sem, device_id={"tp": device}, device_id_type=MESH)


def entry_barrier(place):
    barrier = pltpu.get_barrier_semaphore()
    for peer in (place.core_peer, place.y_peer):
        pl.semaphore_signal(barrier, inc=1, device_id={"tp": peer}, device_id_type=MESH)

    @pl.when(place.z > 0)
    def _():
        pl.semaphore_signal(barrier, inc=1, device_id={"tp": place.down}, device_id_type=MESH)

    @pl.when(place.z < N_Z - 1)
    def _():
        pl.semaphore_signal(barrier, inc=1, device_id={"tp": place.up}, device_id_type=MESH)

    pl.semaphore_wait(barrier, 2 + (place.z + 3) // 4 + (6 - place.z) // 4)


def by_distance(place, dist, act):
    if dist == 0:
        act(place.z)
        return

    @pl.when(place.z + dist < N_Z)
    def _():
        act(place.z + dist)

    @pl.when(place.z >= dist)
    def _():
        act(place.z - dist)


class Gather:
    SEMS = [(4,), (4,), (4,), (4,), (4,), (8,), (8,)]

    def __init__(self, place, own, shard, sems):
        self.place, self.own, self.shard = place, own, shard
        self.up_send, self.down_send, self.z_recv, self.y_send, self.y_recv, self.c_send, self.c_recv = sems

    def src(self, d, k, mine):
        return self.own(k) if mine else self.shard(d, k)

    def to_up(self, zz, k, mine=False):
        d = self.place.index(zz, self.place.y, self.place.c)
        return remote(self.src(d, k, mine), self.shard(d, k), self.up_send.at[k, zz], self.z_recv.at[k, zz], self.place.up)

    def to_down(self, zz, k, mine=False):
        d = self.place.index(zz, self.place.y, self.place.c)
        return remote(self.src(d, k, mine), self.shard(d, k), self.down_send.at[k, zz], self.z_recv.at[k, zz], self.place.down)

    def to_y(self, zz, k, mine=False, flip=False):
        d = self.place.index(zz, 1 - self.place.y if flip else self.place.y, self.place.c)
        return remote(self.src(d, k, mine), self.shard(d, k), self.y_send.at[k, zz], self.y_recv.at[k, zz], self.place.y_peer)

    def to_core(self, zz, yy, k, mine=False, flip=False):
        d = self.place.index(zz, yy, 1 - self.place.c if flip else self.place.c)
        slot = zz * 2 + yy
        return remote(self.src(d, k, mine), self.shard(d, k), self.c_send.at[k, slot], self.c_recv.at[k, slot], self.place.core_peer)

    def stage(self, number, k):
        place = self.place
        z, y = place.z, place.y
        if number == 0:
            @pl.when(z < N_Z - 1)
            def _():
                self.to_up(z, k, True).start()

            @pl.when(z > 0)
            def _():
                self.to_down(z, k, True).start()

            self.to_y(z, k, True).start()
            self.to_core(z, y, k, True).start()
        elif number < N_Z:
            @pl.when(z >= number)
            def _():
                zz = z - number
                self.to_up(zz, k).wait_recv()

                @pl.when(z < N_Z - 1)
                def _():
                    self.to_up(zz, k).start()

                self.to_y(zz, k).start()
                self.to_core(zz, y, k).start()

            @pl.when(z + number < N_Z)
            def _():
                zz = z + number
                self.to_down(zz, k).wait_recv()

                @pl.when(z > 0)
                def _():
                    self.to_down(zz, k).start()

                self.to_y(zz, k).start()
                self.to_core(zz, y, k).start()
        elif number < 2 * N_Z:
            def pass_on(zz):
                self.to_y(zz, k, flip=True).wait_recv()
                self.to_core(zz, 1 - y, k).start()

            by_distance(place, number - N_Z, pass_on)
        else:
            for zz in range(N_Z):
                for yy in range(N_Y):
                    self.to_core(zz, yy, k, flip=True).wait_recv()

    def drain(self, k):
        z = self.place.z
        for zz in range(N_Z):
            @pl.when((z >= zz) & (z < N_Z - 1))
            def _():
                self.to_up(zz, k).wait_send()

            @pl.when((z <= zz) & (z > 0))
            def _():
                self.to_down(zz, k).wait_send()

            self.to_y(zz, k).wait_send()
            for yy in range(N_Y):
                self.to_core(zz, yy, k).wait_send()


class Scatter:
    SEMS = [(8,), (8,), (4,), (4,), (4,), (4,), (4,), (4,)]
    BUFS = (8, 4, 4, 4, 4, 4)

    def __init__(self, place, shard, bufs, total, sems):
        self.place, self.shard, self.total = place, shard, total
        self.c_buf, self.y_out, self.y_in, self.z_out, self.from_down, self.from_up = bufs
        self.c_send, self.c_recv, self.y_send, self.y_recv, self.up_send, self.up_recv, self.down_send, self.down_recv = sems

    def to_core(self, zz, yy, k):
        slot = zz * 2 + yy
        d = self.place.index(zz, yy, 1 - self.place.c)
        return remote(self.shard(d, k), self.c_buf.at[k, slot], self.c_send.at[k, slot], self.c_recv.at[k, slot], self.place.core_peer)

    def to_y(self, zz, k):
        return remote(self.y_out.at[k, zz], self.y_in.at[k, zz], self.y_send.at[k, zz], self.y_recv.at[k, zz], self.place.y_peer)

    def to_up(self, zz, k):
        return remote(self.z_out.at[k, zz], self.from_down.at[k, zz], self.up_send.at[k, zz], self.up_recv.at[k, zz], self.place.up)

    def to_down(self, zz, k):
        return remote(self.z_out.at[k, zz], self.from_up.at[k, zz], self.down_send.at[k, zz], self.down_recv.at[k, zz], self.place.down)

    def pair_sum(self, zz, yy, k):
        self.to_core(zz, yy, k).wait_recv()
        mine = self.shard(self.place.index(zz, yy, self.place.c), k)[...].astype(jnp.float32)
        return mine + self.c_buf[k, zz * 2 + yy].astype(jnp.float32)

    def chip_pair_sum(self, zz, k):
        both = self.pair_sum(zz, self.place.y, k)
        self.to_y(zz, k).wait_recv()
        return both + self.y_in[k, zz].astype(jnp.float32)

    def stage(self, number, k):
        place = self.place
        z, y = place.z, place.y
        if number == 0:
            for yy in (1 - y, y):
                for zz in range(N_Z):
                    self.to_core(zz, yy, k).start()
        elif number == 1:
            def send_y(zz):
                self.y_out[k, zz] = self.pair_sum(zz, 1 - y, k).astype(jnp.bfloat16)
                self.to_y(zz, k).start()

            for dist in (3, 2, 1, 0):
                by_distance(place, dist, send_y)
        elif number < N_STAGES - 1:
            dist = N_STAGES - 1 - number

            @pl.when(z + dist < N_Z)
            def _():
                zz = z + dist
                self.total[...] = self.chip_pair_sum(zz, k)

                @pl.when(z > 0)
                def _():
                    self.to_up(zz, k).wait_recv()
                    self.total[...] += self.from_down[k, zz].astype(jnp.float32)

                self.z_out[k, zz] = self.total[...].astype(jnp.bfloat16)
                self.to_up(zz, k).start()

            @pl.when(z >= dist)
            def _():
                zz = z - dist
                self.total[...] = self.chip_pair_sum(zz, k)

                @pl.when(z < N_Z - 1)
                def _():
                    self.to_down(zz, k).wait_recv()
                    self.total[...] += self.from_up[k, zz].astype(jnp.float32)

                self.z_out[k, zz] = self.total[...].astype(jnp.bfloat16)
                self.to_down(zz, k).start()
        else:
            self.total[...] = self.chip_pair_sum(z, k)

            @pl.when(z > 0)
            def _():
                self.to_up(z, k).wait_recv()
                self.total[...] += self.from_down[k, z].astype(jnp.float32)

            @pl.when(z < N_Z - 1)
            def _():
                self.to_down(z, k).wait_recv()
                self.total[...] += self.from_up[k, z].astype(jnp.float32)

    def drain(self, k):
        z = self.place.z
        for zz in range(N_Z):
            for yy in range(N_Y):
                self.to_core(zz, yy, k).wait_send()
            self.to_y(zz, k).wait_send()

            @pl.when(z < zz)
            def _():
                self.to_up(zz, k).wait_send()

            @pl.when(z > zz)
            def _():
                self.to_down(zz, k).wait_send()


def chunk_sems(kind, n_chunks):
    return [pltpu.SemaphoreType.DMA((n_chunks,) + shape) for shape in kind.SEMS]


def chunk_bufs(n_chunks, rows, width):
    return [pltpu.VMEM((n_chunks, slots, rows, width), jnp.bfloat16) for slots in Scatter.BUFS]


def norm_rows(rows_f32, gain_f32):
    mean_sq = jnp.mean(rows_f32 * rows_f32, axis=-1, keepdims=True)
    return (rows_f32 * lax.rsqrt(mean_sq + NORM_EPS) * gain_f32).astype(jnp.bfloat16)


def scatter_kernel(n_chunks, looked, keep, gain, sum_ref, norm_ref, part, total, *scratch):
    bufs, sems = scratch[:6], scratch[6:]
    rows = total.shape[0]
    place = Place()
    chunk_rows = lambda k: pl.ds(pl.multiple_of(k * rows, rows), rows)
    scat = Scatter(place, lambda d, k: part.at[d, chunk_rows(k), :], bufs, total, sems)
    entry_barrier(place)

    def first(k, carry):
        def mask_rows(d, inner):
            part[d, chunk_rows(k), :] = (looked[d, chunk_rows(k), :].astype(jnp.float32) * keep[d, chunk_rows(k), :]).astype(jnp.bfloat16)
            return inner

        lax.fori_loop(0, part.shape[0], mask_rows, 0)
        scat.stage(0, k)
        return carry

    def second(k, carry):
        scat.stage(1, k)
        return carry

    def finish(k):
        value = total[...].astype(jnp.bfloat16)
        sum_ref[chunk_rows(k), :] = value
        norm_ref[chunk_rows(k), :] = norm_rows(value.astype(jnp.float32), gain[...].astype(jnp.float32))

    def wave(t, carry):
        for number in range(N_STAGES - 1, 1, -1):
            k = t - (number - 2)

            @pl.when((k >= 0) & (k < n_chunks))
            def _():
                scat.stage(number, k)
                if number == N_STAGES - 1:
                    finish(k)
        return carry

    def drain(k, carry):
        scat.drain(k)
        return carry

    lax.fori_loop(0, n_chunks, first, 0)
    lax.fori_loop(0, n_chunks, second, 0)
    lax.fori_loop(0, n_chunks + N_STAGES - 3, wave, 0)
    lax.fori_loop(0, n_chunks, drain, 0)


def scatter_rows(looked, keep, gain, collective_id):
    n_dev = N_Z * N_Y * 2
    width = looked.shape[-1]
    rows_loc = looked.shape[0] // n_dev
    rows = rows_loc // N_CHUNKS
    out = jax.ShapeDtypeStruct((rows_loc, width), jnp.bfloat16)
    return pl.pallas_call(
        functools.partial(scatter_kernel, N_CHUNKS),
        in_specs=[pl.BlockSpec(memory_space=pltpu.VMEM)] * 3,
        out_specs=[pl.BlockSpec(memory_space=pltpu.VMEM)] * 2,
        out_shape=[out, out],
        scratch_shapes=[pltpu.VMEM((n_dev, rows_loc, width), jnp.bfloat16), pltpu.VMEM((rows, width), jnp.float32)] + chunk_bufs(N_CHUNKS, rows, width) + chunk_sems(Scatter, N_CHUNKS),
        compiler_params=pltpu.CompilerParams(collective_id=collective_id, has_side_effects=True, vmem_limit_bytes=VMEM_LIMIT),
        name="scatter_rows",
    )(looked.reshape(n_dev, rows_loc, width), keep.reshape(n_dev, rows_loc, 1), gain.reshape(1, width))


KEY_BLOCK = 512


def attend_kernel(own_ref, wq_ref, wk_ref, wv_ref, qg_ref, kg_ref, cos_ref, sin_ref, out_ref, full, w_all, q_t, k_t, v_t, q_b, k_rows, stat, slots, scores, stat_send, stat_recv, *sems):
    n_dev, rows, width = full.shape
    n_tok = n_dev * rows
    dim = HEAD_DIM
    half = dim // 2
    place = Place()
    me, z, y, c = place.me, place.z, place.y, place.c
    gath = Gather(place, lambda k: own_ref, lambda d, k: full.at[d], sems)
    barrier = pltpu.get_barrier_semaphore()
    for off in range(1, n_dev):
        pl.semaphore_signal(barrier, inc=1, device_id={"tp": (me + off) % n_dev}, device_id_type=MESH)
    pl.semaphore_wait(barrier, n_dev - 1)
    gath.stage(0, 0)
    full[me] = own_ref[...]
    for pos, w_ref in enumerate((wq_ref, wk_ref, wv_ref)):
        w_all[:, pos * dim:(pos + 1) * dim] = w_ref[...]
    packed = jnp.where(z == 0, 228, jnp.where(z == 1, 225, jnp.where(z == 2, 30, 27)))

    def event(e, carry):
        turn, kind = e // 4, e % 4
        rank = turn - (kind + 1) // 2
        valid = (rank >= 0) & (rank < N_Z)
        zz = (packed >> (2 * jnp.clip(rank, 0, N_Z - 1))) & 3

        @pl.when(valid & (kind == 0) & (zz < z))
        def _():
            gath.to_up(zz, 0).wait_recv()

            @pl.when(z < N_Z - 1)
            def _():
                gath.to_up(zz, 0).start()

        @pl.when(valid & (kind == 0) & (zz > z))
        def _():
            gath.to_down(zz, 0).wait_recv()

            @pl.when(z > 0)
            def _():
                gath.to_down(zz, 0).start()

        @pl.when(valid & (kind == 0) & (rank > 0))
        def _():
            gath.to_y(zz, 0).start()
            gath.to_core(zz, y, 0).start()

        @pl.when(valid & (kind == 1))
        def _():
            gath.to_core(zz, y, 0, flip=True).wait_recv()

        @pl.when(valid & (kind == 2))
        def _():
            gath.to_y(zz, 0, flip=True).wait_recv()
            gath.to_core(zz, 1 - y, 0).start()

        @pl.when(valid & (kind == 3))
        def _():
            gath.to_core(zz, 1 - y, 0, flip=True).wait_recv()

        @pl.when(valid)
        def _():
            d = zz * 4 + (y + kind // 2) % 2 * 2 + (c + kind) % 2
            lanes = pl.ds(pl.multiple_of(d * rows, rows), rows)
            qkv = jnp.dot(full[d], w_all[...], preferred_element_type=jnp.float32)
            q_blk, k_blk, v_blk = (qkv[:, i * dim:(i + 1) * dim].T for i in range(3))
            q_t[:, lanes] = q_blk
            k_t[:, lanes] = k_blk
            v_t[:, lanes] = v_blk.astype(jnp.bfloat16)
            stat[0:1, lanes] = jnp.sum(q_blk * q_blk, axis=0, keepdims=True)
            stat[1:2, lanes] = jnp.sum(k_blk * k_blk, axis=0, keepdims=True)
        return carry

    lax.fori_loop(0, 24, event, 0)
    gath.drain(0)

    def to_peer(off):
        return remote(stat, slots.at[me], stat_send.at[off], stat_recv.at[me], (me + off) % n_dev)

    for off in range(1, n_dev):
        to_peer(off).start()
    slots[me] = stat[...]
    for off in range(1, n_dev):
        other = (me + off) % n_dev
        remote(stat, slots.at[other], stat_send.at[off], stat_recv.at[other], other).wait_recv()
    stat_total = jnp.sum(slots[...], axis=0)
    inv_rms = lax.rsqrt(stat_total / (n_dev * dim) + NORM_EPS)
    for off in range(1, n_dev):
        to_peer(off).wait_send()
    slots[0] = inv_rms

    def rotate(blk, carry):
        lanes = pl.ds(pl.multiple_of(blk * KEY_BLOCK, KEY_BLOCK), KEY_BLOCK)
        cos_b, sin_b = cos_ref[:, lanes], sin_ref[:, lanes]
        heads = []
        for row, raw, gain in ((0, q_t, qg_ref), (1, k_t, kg_ref)):
            normed = raw[:, lanes] * slots[0, row:row + 1, lanes] * gain[...]
            first, second = normed[:half], normed[half:]
            heads.append(jnp.concatenate([first * cos_b - second * sin_b, second * cos_b + first * sin_b], axis=0))
        q_b[:, lanes] = heads[0].astype(jnp.bfloat16)
        k_rows[lanes, :] = heads[1].T.astype(jnp.bfloat16)
        return carry

    lax.fori_loop(0, n_tok // KEY_BLOCK, rotate, 0)

    def attend(blk, carry):
        queries = pl.ds(pl.multiple_of(blk * KEY_BLOCK, KEY_BLOCK), KEY_BLOCK)
        q_blk = q_b[:, queries]
        key_rows = lambda j: pl.ds(pl.multiple_of(j * KEY_BLOCK, KEY_BLOCK), KEY_BLOCK)

        def score(j, top):
            raw = jnp.dot(k_rows[key_rows(j), :], q_blk, preferred_element_type=jnp.float32) * (dim ** -0.5)
            key_pos = lax.broadcasted_iota(jnp.int32, raw.shape, 0) + (j - blk) * KEY_BLOCK
            raw = jnp.where(key_pos <= lax.broadcasted_iota(jnp.int32, raw.shape, 1), raw, -1e30)
            scores[key_rows(j), :] = raw
            return jnp.maximum(top, jnp.max(raw, axis=0, keepdims=True))

        top = lax.fori_loop(0, blk + 1, score, jnp.full((1, KEY_BLOCK), -1e30, jnp.float32))

        def expo(j, norm):
            raised = jnp.exp(scores[key_rows(j), :] - top)
            scores[key_rows(j), :] = raised
            return norm + jnp.sum(raised, axis=0, keepdims=True)

        norm = lax.fori_loop(0, blk + 1, expo, jnp.zeros((1, KEY_BLOCK), jnp.float32))
        inv_norm = 1.0 / norm

        def weigh(j, acc):
            prob = (scores[key_rows(j), :] * inv_norm).astype(jnp.bfloat16)
            return acc + jnp.dot(v_t[:, key_rows(j)], prob, preferred_element_type=jnp.float32)

        ctx = lax.fori_loop(0, blk + 1, weigh, jnp.zeros((dim, KEY_BLOCK), jnp.float32)).T.astype(jnp.bfloat16)
        n_chunks = out_ref.shape[0]
        piece = rows // n_chunks
        for dev in range(KEY_BLOCK // rows):
            at = pl.ds(pl.multiple_of((blk * (KEY_BLOCK // rows) + dev) * piece, piece), piece)
            for k in range(n_chunks):
                out_ref[k, at, :] = ctx[dev * rows + k * piece:dev * rows + (k + 1) * piece, :]
        return carry

    lax.fori_loop(0, n_tok // KEY_BLOCK, attend, 0)


def attend_rows(own, wq, wk, wv, q_gain, k_gain, cos_t, sin_t, collective_id):
    n_dev = N_Z * N_Y * 2
    rows, width = own.shape
    n_tok = n_dev * rows
    operands = (own, wq, wk, wv, q_gain, k_gain, cos_t, sin_t)
    return pl.pallas_call(
        attend_kernel,
        in_specs=[pl.BlockSpec(memory_space=pltpu.VMEM)] * len(operands),
        out_specs=pl.BlockSpec(memory_space=pltpu.VMEM),
        out_shape=jax.ShapeDtypeStruct((N_CHUNKS, n_tok // N_CHUNKS, HEAD_DIM), jnp.bfloat16),
        scratch_shapes=[
            pltpu.VMEM((n_dev, rows, width), jnp.bfloat16),
            pltpu.VMEM((width, 3 * HEAD_DIM), jnp.bfloat16),
            pltpu.VMEM((HEAD_DIM, n_tok), jnp.float32),
            pltpu.VMEM((HEAD_DIM, n_tok), jnp.float32),
            pltpu.VMEM((HEAD_DIM, n_tok), jnp.bfloat16),
            pltpu.VMEM((HEAD_DIM, n_tok), jnp.bfloat16),
            pltpu.VMEM((n_tok, HEAD_DIM), jnp.bfloat16),
            pltpu.VMEM((2, n_tok), jnp.float32),
            pltpu.VMEM((n_dev, 2, n_tok), jnp.float32),
            pltpu.VMEM((n_tok, KEY_BLOCK), jnp.float32),
            pltpu.SemaphoreType.DMA((n_dev,)),
            pltpu.SemaphoreType.DMA((n_dev,)),
        ] + chunk_sems(Gather, 1),
        compiler_params=pltpu.CompilerParams(collective_id=collective_id, has_side_effects=True, vmem_limit_bytes=VMEM_LIMIT),
        name="attend_rows",
    )(*operands)


SUM_STEPS = {0: 0, 1: 1, 3: 2, 4: 3, 5: 4, 6: 5}


def moe_kernel(n_chunks, exp_step, ctx_ref, wo_ref, x_ref, gain_ref, mask_ref, wr_ref, wg_ref, wu_ref, wd_ref, out_ref, acc_ref, gate_ref, full, part, total, m_own, h_own, *rest):
    bufs, rest = rest[:6], rest[6:]
    n_sc = len(Scatter.SEMS)
    attn_sems, moe_sems, gather_sems = rest[:n_sc], rest[n_sc:2 * n_sc], rest[2 * n_sc:]
    chunk, step = pl.program_id(0), pl.program_id(1)
    n_steps = pl.num_programs(1)
    rows = m_own.shape[0] // n_chunks
    n_exp = wr_ref.shape[0]
    exp_ff = wg_ref.shape[0] // exp_step
    n_tok = full.shape[1]
    nt_dims = (((1,), (1,)), ((), ()))
    place = Place()
    loc_rows = lambda k: pl.ds(pl.multiple_of(k * rows, rows), rows)
    block = lambda ref: (lambda d, k: ref.at[k, pl.ds(pl.multiple_of(d * rows, rows), rows), :])
    gath = Gather(place, lambda k: m_own.at[loc_rows(k), :], block(full), gather_sems)
    attn = Scatter(place, block(part), bufs, total, attn_sems)
    scat = Scatter(place, block(part), bufs, total, moe_sems)

    def project(k):
        part[k] = jnp.dot(ctx_ref[k], wo_ref[...], preferred_element_type=jnp.float32).astype(jnp.bfloat16)

    def attn_stage(number, k):
        attn.stage(number, k)
        if number == N_STAGES - 1:
            attn_out = total[...].astype(jnp.bfloat16).astype(jnp.float32)
            hidden = (x_ref[loc_rows(k), :].astype(jnp.float32) + attn_out).astype(jnp.bfloat16)
            h_own[loc_rows(k), :] = hidden
            normed = norm_rows(hidden.astype(jnp.float32), gain_ref[...].astype(jnp.float32))
            m_own[loc_rows(k), :] = normed
            full[k, pl.ds(pl.multiple_of(place.me * rows, rows), rows), :] = normed

    def moe_stage(number, k):
        scat.stage(number, k)
        if number == N_STAGES - 1:
            moe_out = total[...].astype(jnp.bfloat16).astype(jnp.float32)
            out_ref[loc_rows(k), :] = (h_own[loc_rows(k), :].astype(jnp.float32) + moe_out).astype(jnp.bfloat16)

    @pl.when((chunk == 0) & (step == 0))
    def _():
        entry_barrier(place)
        for k in (0, 1):
            project(k)
            attn_stage(0, k)
        attn_stage(1, 0)
        for k in range(2, n_chunks):
            project(k)
            attn_stage(0, k)
        attn_stage(1, 1)
        for number in range(2, N_STAGES):
            attn_stage(number, 0)
        attn_stage(2, 1)
        gath.stage(0, 0)
        attn_stage(3, 1)
        for number in (1, 4):
            gath.stage(number, 0)
        attn_stage(4, 1)
        for number in (2, 5):
            gath.stage(number, 0)
        attn_stage(5, 1)
        for number in (3, 6, 7, 8):
            gath.stage(number, 0)

    for at in range(2 * N_Z):
        @pl.when((step == at) & (chunk + 1 < n_chunks))
        def _():
            gath.stage(at, chunk + 1)

        if at in SUM_STEPS:
            @pl.when((step == at) & (chunk > 0))
            def _():
                moe_stage(SUM_STEPS[at], chunk - 1)

            if at > 0:
                @pl.when((step == at) & (chunk == 0))
                def _():
                    attn_stage(SUM_STEPS[at], 2)

    for at_chunk, at, number in ((0, 5, 1), (0, 7, 2), (1, 0, 3), (1, 1, 4), (1, 2, 5)):
        @pl.when((step == at) & (chunk == at_chunk))
        def _():
            attn_stage(number, 3)

    @pl.when((step == 0) & (chunk > 0))
    def _():
        gath.stage(GATHER_LAST, chunk)

    @pl.when(step == 0)
    def _():
        logits = lax.dot_general(full[chunk], wr_ref[...], nt_dims, preferred_element_type=jnp.float32)
        logits = logits - jnp.max(logits, axis=-1, keepdims=True)
        expd = jnp.exp(logits)
        gates = expd / jnp.sum(expd, axis=-1, keepdims=True) * mask_ref[0]
        for grp in range(n_exp // exp_step):
            gate_ref[grp] = gates[:, grp * exp_step:(grp + 1) * exp_step]
        acc_ref[...] = jnp.zeros_like(acc_ref)

    m_rows = full[chunk]
    gate_proj = lax.dot_general(m_rows, wg_ref[...], nt_dims, preferred_element_type=jnp.float32)
    up_proj = lax.dot_general(m_rows, wu_ref[...], nt_dims, preferred_element_type=jnp.float32)
    act = (gate_proj / (1.0 + jnp.exp(-gate_proj)) * up_proj).astype(jnp.bfloat16).astype(jnp.float32)
    gates = gate_ref[step]
    lane = lax.broadcasted_iota(jnp.int32, (n_tok, 2 * exp_ff), 1)
    pieces = []
    for pair in range(exp_step // 2):
        pieces.append(jnp.where(lane < exp_ff, gates[:, 2 * pair:2 * pair + 1], gates[:, 2 * pair + 1:2 * pair + 2]))
    scaled = act * jnp.concatenate(pieces, axis=1)
    high = scaled.astype(jnp.bfloat16)
    low = (scaled - high.astype(jnp.float32)).astype(jnp.bfloat16)
    acc_ref[...] += jnp.dot(high, wd_ref[...], preferred_element_type=jnp.float32) + jnp.dot(low, wd_ref[...], preferred_element_type=jnp.float32)

    @pl.when(step == n_steps - 1)
    def _():
        attn.drain(chunk)
        part[chunk] = acc_ref[...].astype(jnp.bfloat16)

    @pl.when((step == n_steps - 1) & (chunk == n_chunks - 1))
    def _():
        for number in range(N_STAGES):
            moe_stage(number, n_chunks - 1)

        def drain(k, carry):
            gath.drain(k)
            scat.drain(k)
            return carry

        lax.fori_loop(0, n_chunks, drain, 0)


def moe_layer(ctx, w_out, x_loc, gain, mask, wr_t, wg_t, wu_t, w_dn, collective_id):
    rows_loc, width = x_loc.shape
    n_chunks, n_tok, n_exp = mask.shape
    n_ff = wg_t.shape[0]
    step_cols = n_ff // n_exp * EXP_PER_STEP
    rows = rows_loc // n_chunks
    const = lambda k, s: (0, 0)
    return pl.pallas_call(
        functools.partial(moe_kernel, n_chunks, EXP_PER_STEP),
        grid=(n_chunks, n_ff // step_cols),
        in_specs=[
            pl.BlockSpec(ctx.shape, lambda k, s: (0, 0, 0)),
            pl.BlockSpec(w_out.shape, const),
            pl.BlockSpec((rows_loc, width), const),
            pl.BlockSpec((1, width), const),
            pl.BlockSpec((1, n_tok, n_exp), lambda k, s: (k, 0, 0)),
            pl.BlockSpec((n_exp, width), const),
            pl.BlockSpec((step_cols, width), lambda k, s: (s, 0)),
            pl.BlockSpec((step_cols, width), lambda k, s: (s, 0)),
            pl.BlockSpec((step_cols, width), lambda k, s: (s, 0)),
        ],
        out_specs=pl.BlockSpec((rows_loc, width), const),
        out_shape=jax.ShapeDtypeStruct((rows_loc, width), jnp.bfloat16),
        scratch_shapes=[
            pltpu.VMEM((n_tok, width), jnp.float32),
            pltpu.VMEM((n_exp // EXP_PER_STEP, n_tok, EXP_PER_STEP), jnp.float32),
            pltpu.VMEM((n_chunks, n_tok, width), jnp.bfloat16),
            pltpu.VMEM((n_chunks, n_tok, width), jnp.bfloat16),
            pltpu.VMEM((rows, width), jnp.float32),
            pltpu.VMEM((rows_loc, width), jnp.bfloat16),
            pltpu.VMEM((rows_loc, width), jnp.bfloat16),
        ] + chunk_bufs(n_chunks, rows, width) + chunk_sems(Scatter, n_chunks) + chunk_sems(Scatter, n_chunks) + chunk_sems(Gather, n_chunks),
        compiler_params=pltpu.CompilerParams(dimension_semantics=("arbitrary", "arbitrary"), collective_id=collective_id, has_side_effects=True, vmem_limit_bytes=VMEM_LIMIT),
        name="moe_layer",
    )(ctx, w_out, x_loc, gain.reshape(1, width), mask, wr_t, wg_t, wu_t, w_dn)


def solution(mesh):
    tp_size = mesh.shape["tp"]
    in_specs = (P("dp", None), P("dp", None, None), P("tp", None), P(None), P(None, "tp"), P(None, "tp"), P(None, "tp"), P("tp", None), P("tp"), P("tp"), P(None), P(None, None), P(None, None, "tp"), P(None, None, "tp"), P(None, "tp", None))

    def device_fn(token_ids, route_idx, embed_table, attn_norm, w_query, w_key, w_value, w_out, q_gain, k_gain, mlp_norm, w_router, w_gate, w_up, w_down):
        batch_loc, seq_len = token_ids.shape
        vocab_loc, model_dim = embed_table.shape
        tp_rank = lax.axis_index("tp")
        local_ids = token_ids - tp_rank * vocab_loc
        in_range = (local_ids >= 0) & (local_ids < vocab_loc)
        looked_up = jnp.take(embed_table, jnp.clip(local_ids, 0, vocab_loc - 1).reshape(-1), axis=0, mode="clip")
        x_loc, a_loc = scatter_rows(looked_up, in_range.astype(jnp.float32), attn_norm, 0)
        cos_tab, sin_tab = rope_tables(seq_len)
        as_column = lambda gain: gain.astype(jnp.float32).reshape(-1, 1)
        context = attend_rows(a_loc, w_query, w_key, w_value, as_column(q_gain), as_column(k_gain), cos_tab.T, sin_tab.T, 1)
        n_exp = w_gate.shape[0]
        wg_t = jnp.swapaxes(w_gate, 1, 2).reshape(-1, model_dim)
        wu_t = jnp.swapaxes(w_up, 1, 2).reshape(-1, model_dim)
        w_dn = w_down.reshape(-1, model_dim)
        wr_t = w_router.T
        expert_iota = jnp.arange(n_exp, dtype=jnp.int32)
        chosen = route_idx.reshape(batch_loc * seq_len, -1)
        mask = jnp.any(chosen[:, :, None] == expert_iota[None, None, :], axis=1).astype(jnp.float32)
        rows_chunk = x_loc.shape[0] // N_CHUNKS
        to_chunks = lambda arr: arr.reshape(tp_size, N_CHUNKS, rows_chunk, -1).swapaxes(0, 1).reshape(N_CHUNKS, tp_size * rows_chunk, -1)
        out_loc = moe_layer(context, w_out, x_loc, mlp_norm, to_chunks(mask), wr_t, wg_t, wu_t, w_dn, 4)
        return out_loc.reshape(batch_loc, -1, model_dim)

    return jax.shard_map(device_fn, mesh=mesh, in_specs=in_specs, out_specs=P("dp", "tp", None), check_vma=False)
```

profile of v0, /device:TPU:0, one launch (start us, length us, event | category | flops | bytes accessed | tf_op | source)
XLA Modules:
  0.0 428.1 jit_solution(16104885629920499445)
XLA Ops:
  0.0 0.7 subtract_clamp_fusion
  0.7 0.0 copy-start.1
  0.7 0.0 copy-start.2
  0.8 22.7 %gather_fusion = bf16[2048,2048]{1,0:T(8,128)(2,1)} fusion(bf16[3144,2048]{1,0:T(8,128)(2,1)} %param.17, s32[2048]{0:T(1024)S(1)} %broadcast_clamp_fusion), kind=kCustom, calls=%fused_computation | custom fusion | bytes 16785408 | tf_op jit(solution)/shard_map/jit(_take)/gather | solution.py:703
  23.4 0.0 copy-start.4
  23.4 0.0 copy-start.5
  23.4 0.0 copy-start
  23.4 0.0 copy-done.1
  23.5 1.4 copy.24.keep
  24.9 0.0 copy-done.2
  24.9 0.6 reshape.57.gain
  25.5 0.0 copy-start.3
  25.5 69.3 %scatter_rows.1 = (bf16[128,2048]{1,0:T(8,128)(2,1)}, bf16[128,2048]{1,0:T(8,128)(2,1)}) custom-call(bf16[16,128,2048]{2,1,0:T(8,128)(2,1)} %bitcast.23, f32[16,128,1]{2,1,0:T(8,128)} %copy.24.keep, bf16[1,2048]{1,0:T(2,128)(2,1)} %reshape.57.gain), custom_call_target="tpu_custom_call" | custom-call | tf_op jit(solution)/shard_map/scatter_rows/pallas_call | solution.py:341
  94.8 2.8 fusion.1
  97.6 0.0 copy-done.4
  97.6 0.7 copy.25.qg_ref
  98.3 0.0 copy-done.5
  98.4 0.7 copy.26.kg_ref
  99.1 72.8 %attend_rows.1.ctx_ref = bf16[4,512,128]{2,1,0:T(8,128)(2,1)} custom-call(bf16[128,2048]{1,0:T(8,128)(2,1)} %get-tuple-element.7.own_ref, bf16[2048,128]{1,0:T(8,128)(2,1)} %wq_ref.1, bf16[2048,128]{1,0:T(8,128)(2,1)} %wk_ref.1, bf16[2048,128]{1,0:T(8,128)(2,1)} %wv_ref.1, f32[128,1]{1,0:T(8,128)} %copy.25.qg_ref, f32[128,1]{1,0:T(8,128)} %copy.26.kg_ref, ...), custom_call_target="tpu_custom_call" | custom-call | tf_op jit(solution)/shard_map/attend_rows/pallas_call | solution.py:501
  171.9 0.0 copy-done
  171.9 0.7 fusion
  172.6 0.3 copy.27
  173.0 1.1 copy.28
  174.1 0.0 copy-done.3
  174.1 0.6 reshape.62.gain_ref
  174.7 251.6 %moe_layer.1 = bf16[128,2048]{1,0:T(8,128)(2,1)} custom-call(bf16[4,512,128]{2,1,0:T(8,128)(2,1)} %attend_rows.1.ctx_ref, bf16[128,2048]{1,0:T(8,128)(2,1)} %wo_ref.1, bf16[128,2048]{1,0:T(8,128)(2,1)} %get-tuple-element.8.x_ref, bf16[1,2048]{1,0:T(2,128)(2,1)} %reshape.62.gain_ref, f32[4,512,64]{2,1,0:T(8,128)} %bitcast.27, bf16[64,2048]{1,0:T(8,128)(2,1)} %bitcast.30, ...), custom_call_target="tpu_custom_call" | custom-call | tf_op jit(solution)/shard_map/moe_layer/pallas_call | solution.py:663
  426.3 1.9 copy.30
  (6 shorter events, 0.1 us)
Async XLA Ops:
  0.7 22.7 %copy-start.1 = (s32[1,2048]{1,0:T(1,128)S(1)}, s32[1,2048]{1,0:T(1,128)}, u32[]{:S(2)}) copy-start(s32[1,2048]{1,0:T(1,128)} %param.15) | copy-start | bytes 24580
  0.7 24.2 %copy-start.2 = (bf16[2048]{0:T(1024)(128)(2,1)S(1)}, bf16[2048]{0:T(1024)(128)(2,1)}, u32[]{:S(2)}) copy-start(bf16[2048]{0:T(1024)(128)(2,1)} %param.18) | copy-start | bytes 12292
  23.4 74.2 %copy-start.4 = (bf16[128]{0:T(256)(128)(2,1)S(1)}, bf16[128]{0:T(256)(128)(2,1)}, u32[]{:S(2)}) copy-start(bf16[128]{0:T(256)(128)(2,1)} %param.23) | copy-start | bytes 772
  23.4 74.9 %copy-start.5 = (bf16[128]{0:T(256)(128)(2,1)S(1)}, bf16[128]{0:T(256)(128)(2,1)}, u32[]{:S(2)}) copy-start(bf16[128]{0:T(256)(128)(2,1)} %param.24) | copy-start | bytes 772
  23.4 148.5 %copy-start = (s32[1,2048,8]{1,2,0:T(8,128)S(1)}, s32[1,2048,8]{1,2,0:T(8,128)}, u32[]{:S(2)}) copy-start(s32[1,2048,8]{1,2,0:T(8,128)} %param.16) | copy-start | bytes 196612
  25.5 148.6 %copy-start.3 = (bf16[2048]{0:T(1024)(128)(2,1)S(1)}, bf16[2048]{0:T(1024)(128)(2,1)}, u32[]{:S(2)}) copy-start(bf16[2048]{0:T(1024)(128)(2,1)} %param.25) | copy-start | bytes 12292
where the time goes:
time: 428 us
  Pallas kernels  394 us (92%)
  local copies, waits for them, and re-layouts  30.1 us (7%)
  other arithmetic  4.29 us (1%)
    pallas_call x1, Pallas kernels, moe_layer(): pl.pallas_call(functools.partial(moe_kernel, n_chunks, EXP_PER_STEP), gri...  252 us
    pallas_call x1, Pallas kernels, attend_rows(): pl.pallas_call(attend_kernel, in_specs=[pl.BlockSpec(memory_space=pltpu.V...  72.8 us
    pallas_call x1, Pallas kernels, scatter_rows(): pl.pallas_call(functools.partial(scatter_kernel, N_CHUNKS), in_specs=[pl....  69.3 us
    gather x1, local copies, waits for them, and re-layouts, device_fn(): jnp.take(embed_table, jnp.clip(local_ids, 0, vocab_loc - 1).reshape(-1),...  22.7 us

commit v1 on v0

--- a/solution.py
+++ b/solution.py
@@ -2,6 +2,7 @@
 
 import jax
 import jax.numpy as jnp
+import numpy as np
 from jax import lax
 from jax.experimental import pallas as pl
 from jax.experimental.pallas import tpu as pltpu
@@ -16,12 +17,14 @@
 
 def rope_tables(seq_len):
     half_dim = HEAD_DIM // 2
-    inv_freq = 1.0 / (10000.0 ** (jnp.arange(half_dim, dtype=jnp.float32) * (2.0 / HEAD_DIM)))
-    angles = jnp.arange(seq_len, dtype=jnp.float32)[:, None] * inv_freq[None, :]
-    return jnp.cos(angles), jnp.sin(angles)
+    inv_freq = np.float32(1.0) / (np.float32(10000.0) ** (np.arange(half_dim, dtype=np.float32) * np.float32(2.0 / HEAD_DIM)))
+    angles = (inv_freq[:, None] * np.arange(seq_len, dtype=np.float32)[None, :]).astype(np.float32)
+    return np.cos(angles).astype(np.float32), np.sin(angles).astype(np.float32)
 
 
 N_STAGES = 6
+DOWN_COLS = 256
+HOT_COLS = 256
 N_Z, N_Y = 4, 2
 GATHER_LAST = 8
 MESH = pl.DeviceIdType.MESH
@@ -285,26 +288,35 @@
     return (rows_f32 * lax.rsqrt(mean_sq + NORM_EPS) * gain_f32).astype(jnp.bfloat16)
 
 
-def scatter_kernel(n_chunks, looked, keep, gain, sum_ref, norm_ref, part, total, *scratch):
+def scatter_kernel(n_chunks, ids_ref, gain, table_ref, sum_ref, norm_ref, table, hot, part, total, table_sem, *scratch):
     bufs, sems = scratch[:6], scratch[6:]
     rows = total.shape[0]
+    n_tok, vocab_pad = hot.shape
+    vocab = table_ref.shape[0]
+    width = table.shape[1]
+    lanes = 128
     place = Place()
     chunk_rows = lambda k: pl.ds(pl.multiple_of(k * rows, rows), rows)
-    scat = Scatter(place, lambda d, k: part.at[d, chunk_rows(k), :], bufs, total, sems)
+    scat = Scatter(place, lambda d, k: part.at[k, pl.ds(pl.multiple_of(d * rows, rows), rows), :], bufs, total, sems)
+    load = pltpu.make_async_copy(table_ref, table.at[pl.ds(0, vocab), :], table_sem)
+    load.start()
+    table[vocab:, :] = jnp.zeros((vocab_pad - vocab, width), jnp.bfloat16)
     entry_barrier(place)
 
-    def first(k, carry):
-        def mask_rows(d, inner):
-            part[d, chunk_rows(k), :] = (looked[d, chunk_rows(k), :].astype(jnp.float32) * keep[d, chunk_rows(k), :]).astype(jnp.bfloat16)
+    def look_up(k):
+        ids = jnp.broadcast_to(ids_ref[k], (lanes, n_tok)).T - place.me * vocab
+        lane = lax.broadcasted_iota(jnp.int32, (n_tok, lanes), 1)
+        for col in range(0, vocab_pad, lanes):
+            in_table = lane + col < vocab if col + lanes > vocab else True
+            hot[:, col:col + lanes] = jnp.where((ids == lane + col) & in_table, 1.0, 0.0).astype(jnp.bfloat16)
+
+    def product(k):
+        def columns(n, inner):
+            cols = pl.ds(pl.multiple_of(n * HOT_COLS, HOT_COLS), HOT_COLS)
+            part[k, :, cols] = jnp.dot(hot[...], table[:, cols], preferred_element_type=jnp.float32).astype(jnp.bfloat16)
             return inner
 
-        lax.fori_loop(0, part.shape[0], mask_rows, 0)
-        scat.stage(0, k)
-        return carry
-
-    def second(k, carry):
-        scat.stage(1, k)
-        return carry
+        lax.fori_loop(0, width // HOT_COLS, columns, 0)
 
     def finish(k):
         value = total[...].astype(jnp.bfloat16)
@@ -313,40 +325,61 @@
 
     def wave(t, carry):
         for number in range(N_STAGES - 1, 1, -1):
-            k = t - (number - 2)
+            k = t - number
 
             @pl.when((k >= 0) & (k < n_chunks))
             def _():
                 scat.stage(number, k)
                 if number == N_STAGES - 1:
                     finish(k)
+
+        @pl.when((t >= 1) & (t - 1 < n_chunks))
+        def _():
+            scat.stage(1, t - 1)
+
+        @pl.when(t < n_chunks)
+        def _():
+            look_up(t)
+
+            @pl.when(t == 0)
+            def _():
+                load.wait()
+
+            product(t)
+            scat.stage(0, t)
         return carry
 
     def drain(k, carry):
         scat.drain(k)
         return carry
 
-    lax.fori_loop(0, n_chunks, first, 0)
-    lax.fori_loop(0, n_chunks, second, 0)
-    lax.fori_loop(0, n_chunks + N_STAGES - 3, wave, 0)
+    lax.fori_loop(0, n_chunks + N_STAGES - 1, wave, 0)
     lax.fori_loop(0, n_chunks, drain, 0)
 
 
-def scatter_rows(looked, keep, gain, collective_id):
+def scatter_rows(ids, table, gain, collective_id):
     n_dev = N_Z * N_Y * 2
-    width = looked.shape[-1]
-    rows_loc = looked.shape[0] // n_dev
-    rows = rows_loc // N_CHUNKS
-    out = jax.ShapeDtypeStruct((rows_loc, width), jnp.bfloat16)
+    vocab, width = table.shape
+    n_chunks, _, n_tok = ids.shape
+    rows = n_tok // n_dev
+    vocab_pad = -(-vocab // 256) * 256
+    out = jax.ShapeDtypeStruct((n_chunks * rows, width), jnp.bfloat16)
+    vmem = pl.BlockSpec(memory_space=pltpu.VMEM)
     return pl.pallas_call(
-        functools.partial(scatter_kernel, N_CHUNKS),
-        in_specs=[pl.BlockSpec(memory_space=pltpu.VMEM)] * 3,
-        out_specs=[pl.BlockSpec(memory_space=pltpu.VMEM)] * 2,
+        functools.partial(scatter_kernel, n_chunks),
+        in_specs=[vmem, vmem, pl.BlockSpec(memory_space=pl.ANY)],
+        out_specs=[vmem] * 2,
         out_shape=[out, out],
-        scratch_shapes=[pltpu.VMEM((n_dev, rows_loc, width), jnp.bfloat16), pltpu.VMEM((rows, width), jnp.float32)] + chunk_bufs(N_CHUNKS, rows, width) + chunk_sems(Scatter, N_CHUNKS),
+        scratch_shapes=[
+            pltpu.VMEM((vocab_pad, width), jnp.bfloat16),
+            pltpu.VMEM((n_tok, vocab_pad), jnp.bfloat16),
+            pltpu.VMEM((n_chunks, n_tok, width), jnp.bfloat16),
+            pltpu.VMEM((rows, width), jnp.float32),
+            pltpu.SemaphoreType.DMA,
+        ] + chunk_bufs(n_chunks, rows, width) + chunk_sems(Scatter, n_chunks),
         compiler_params=pltpu.CompilerParams(collective_id=collective_id, has_side_effects=True, vmem_limit_bytes=VMEM_LIMIT),
         name="scatter_rows",
-    )(looked.reshape(n_dev, rows_loc, width), keep.reshape(n_dev, rows_loc, 1), gain.reshape(1, width))
+    )(ids, gain.reshape(1, width), table)
 
 
 KEY_BLOCK = 512
@@ -633,7 +666,11 @@
     scaled = act * jnp.concatenate(pieces, axis=1)
     high = scaled.astype(jnp.bfloat16)
     low = (scaled - high.astype(jnp.float32)).astype(jnp.bfloat16)
-    acc_ref[...] += jnp.dot(high, wd_ref[...], preferred_element_type=jnp.float32) + jnp.dot(low, wd_ref[...], preferred_element_type=jnp.float32)
+    both = jnp.concatenate([high, low], axis=0)
+    for col in range(0, acc_ref.shape[1], DOWN_COLS):
+        cols = slice(col, col + DOWN_COLS)
+        down = jnp.dot(both, wd_ref[:, cols], preferred_element_type=jnp.float32)
+        acc_ref[:, cols] += down[:n_tok] + down[n_tok:]
 
     @pl.when(step == n_steps - 1)
     def _():
@@ -696,15 +733,12 @@
 
     def device_fn(token_ids, route_idx, embed_table, attn_norm, w_query, w_key, w_value, w_out, q_gain, k_gain, mlp_norm, w_router, w_gate, w_up, w_down):
         batch_loc, seq_len = token_ids.shape
-        vocab_loc, model_dim = embed_table.shape
-        tp_rank = lax.axis_index("tp")
-        local_ids = token_ids - tp_rank * vocab_loc
-        in_range = (local_ids >= 0) & (local_ids < vocab_loc)
-        looked_up = jnp.take(embed_table, jnp.clip(local_ids, 0, vocab_loc - 1).reshape(-1), axis=0, mode="clip")
-        x_loc, a_loc = scatter_rows(looked_up, in_range.astype(jnp.float32), attn_norm, 0)
-        cos_tab, sin_tab = rope_tables(seq_len)
+        model_dim = embed_table.shape[1]
+        ids = token_ids.reshape(tp_size, N_CHUNKS, -1).swapaxes(0, 1).reshape(N_CHUNKS, 1, -1)
+        x_loc, a_loc = scatter_rows(ids, embed_table, attn_norm, 0)
+        cos_t, sin_t = (jnp.asarray(tab) for tab in rope_tables(seq_len))
         as_column = lambda gain: gain.astype(jnp.float32).reshape(-1, 1)
-        context = attend_rows(a_loc, w_query, w_key, w_value, as_column(q_gain), as_column(k_gain), cos_tab.T, sin_tab.T, 1)
+        context = attend_rows(a_loc, w_query, w_key, w_value, as_column(q_gain), as_column(k_gain), cos_t, sin_t, 1)
         n_exp = w_gate.shape[0]
         wg_t = jnp.swapaxes(w_gate, 1, 2).reshape(-1, model_dim)
         wu_t = jnp.swapaxes(w_up, 1, 2).reshape(-1, model_dim)

time: 428 us -> 421 us (0.984)
  local copies, waits for them, and re-layouts: 30.1 us -> 8.61 us
  Pallas kernels: 394 us -> 408 us
    gather x1 -> x0, local copies, waits for them, and re-layouts: 22.7 us -> none  [device_fn(): jnp.take(embed_table, jnp.clip(local_ids, 0, vocab_loc - 1).reshape(-1),...]
    pallas_call x1, Pallas kernels: 69.3 us -> 80.6 us  [scatter_rows(): pl.pallas_call(functools.partial(scatter_kernel, n_chunks), in_specs=[vme...]
where the time goes in v1:
time: 421 us
  Pallas kernels  408 us (97%)
  local copies, waits for them, and re-layouts  8.61 us (2%)
    pallas_call x1, Pallas kernels, moe_layer(): pl.pallas_call(functools.partial(moe_kernel, n_chunks, EXP_PER_STEP), gri...  254 us
    pallas_call x1, Pallas kernels, scatter_rows(): pl.pallas_call(functools.partial(scatter_kernel, n_chunks), in_specs=[vme...  80.6 us
    pallas_call x1, Pallas kernels, attend_rows(): pl.pallas_call(attend_kernel, in_specs=[pl.BlockSpec(memory_space=pltpu.V...  73.3 us

profile of v1, /device:TPU:0, one launch (start us, length us, event | category | flops | bytes accessed | tf_op | source)
XLA Modules:
  0.0 420.5 jit_solution(2463049968525823902)
XLA Ops:
  0.0 0.7 bitcast_convert_fusion.1
  0.7 0.7 bitcast_convert_fusion
  1.3 0.5 broadcast.3
  1.8 1.4 reduce.3
  3.2 1.3 reshape.46.gain
  4.5 1.3 reshape.51.gain_ref
  5.8 0.1 reshape.44
  5.9 0.7 reshape.45.ids_ref
  6.5 0.7 copy.29.kg_ref
  7.3 0.7 copy.28.qg_ref
  8.0 1.4 fusion
  9.4 0.3 copy.30
  9.8 1.1 copy.31
  10.8 80.6 %scatter_rows.1 = (bf16[128,2048]{1,0:T(8,128)(2,1)}, bf16[128,2048]{1,0:T(8,128)(2,1)}) custom-call(s32[4,1,512]{2,1,0:T(1,128)} %reshape.45.ids_ref, bf16[1,2048]{1,0:T(2,128)(2,1)} %reshape.46.gain, bf16[3144,2048]{1,0:T(8,128)(2,1)} %table_ref.1), custom_call_target="tpu_custom_call" | custom-call | tf_op jit(solution)/shard_map/scatter_rows/pallas_call | solution.py:368
  91.5 73.3 %attend_rows.1.ctx_ref = bf16[4,512,128]{2,1,0:T(8,128)(2,1)} custom-call(bf16[128,2048]{1,0:T(8,128)(2,1)} %get-tuple-element.7.own_ref, bf16[2048,128]{1,0:T(8,128)(2,1)} %wq_ref.1, bf16[2048,128]{1,0:T(8,128)(2,1)} %wk_ref.1, bf16[2048,128]{1,0:T(8,128)(2,1)} %wv_ref.1, f32[128,1]{1,0:T(8,128)} %copy.28.qg_ref, f32[128,1]{1,0:T(8,128)} %copy.29.kg_ref, ...), custom_call_target="tpu_custom_call" | custom-call | tf_op jit(solution)/shard_map/attend_rows/pallas_call | solution.py:534
  164.8 253.8 %moe_layer.1 = bf16[128,2048]{1,0:T(8,128)(2,1)} custom-call(bf16[4,512,128]{2,1,0:T(8,128)(2,1)} %attend_rows.1.ctx_ref, bf16[128,2048]{1,0:T(8,128)(2,1)} %wo_ref.1, bf16[128,2048]{1,0:T(8,128)(2,1)} %get-tuple-element.8.x_ref, bf16[1,2048]{1,0:T(2,128)(2,1)} %reshape.51.gain_ref, f32[4,512,64]{2,1,0:T(8,128)} %bitcast.26, bf16[64,2048]{1,0:T(8,128)(2,1)} %bitcast.29, ...), custom_call_target="tpu_custom_call" | custom-call | tf_op jit(solution)/shard_map/moe_layer/pallas_call | solution.py:700
  418.6 1.9 copy.35
  (2 shorter events, 0.0 us)

commit v2 on v1

--- a/solution.py
+++ b/solution.py
@@ -10,7 +10,7 @@
 
 HEAD_DIM = 128
 NORM_EPS = 1e-5
-N_CHUNKS = 4
+N_CHUNKS = 8
 EXP_PER_STEP = 8
 VMEM_LIMIT = 63 * 1024 * 1024
 
@@ -288,7 +288,7 @@
     return (rows_f32 * lax.rsqrt(mean_sq + NORM_EPS) * gain_f32).astype(jnp.bfloat16)
 
 
-def scatter_kernel(n_chunks, ids_ref, gain, table_ref, sum_ref, norm_ref, table, hot, part, total, table_sem, *scratch):
+def scatter_kernel(n_chunks, ids_ref, gain, table_ref, sum_ref, norm_ref, table, hot, part, total, id_cols, table_sem, *scratch):
     bufs, sems = scratch[:6], scratch[6:]
     rows = total.shape[0]
     n_tok, vocab_pad = hot.shape
@@ -300,11 +300,14 @@
     scat = Scatter(place, lambda d, k: part.at[k, pl.ds(pl.multiple_of(d * rows, rows), rows), :], bufs, total, sems)
     load = pltpu.make_async_copy(table_ref, table.at[pl.ds(0, vocab), :], table_sem)
     load.start()
+    for d in range(n_tok // rows):
+        span = slice(d * rows * n_chunks, (d + 1) * rows * n_chunks)
+        id_cols[d] = jnp.broadcast_to(ids_ref[:, span], (lanes, rows * n_chunks)).T
     table[vocab:, :] = jnp.zeros((vocab_pad - vocab, width), jnp.bfloat16)
     entry_barrier(place)
 
     def look_up(k):
-        ids = jnp.broadcast_to(ids_ref[k], (lanes, n_tok)).T - place.me * vocab
+        ids = jnp.concatenate([id_cols[d, chunk_rows(k), :] for d in range(n_tok // rows)], axis=0) - place.me * vocab
         lane = lax.broadcasted_iota(jnp.int32, (n_tok, lanes), 1)
         for col in range(0, vocab_pad, lanes):
             in_table = lane + col < vocab if col + lanes > vocab else True
@@ -321,7 +324,7 @@
     def finish(k):
         value = total[...].astype(jnp.bfloat16)
         sum_ref[chunk_rows(k), :] = value
-        norm_ref[chunk_rows(k), :] = norm_rows(value.astype(jnp.float32), gain[...].astype(jnp.float32))
+        norm_ref[chunk_rows(k), :] = norm_rows(value.astype(jnp.float32), gain[...].astype(jnp.float32).reshape(1, -1))
 
     def wave(t, carry):
         for number in range(N_STAGES - 1, 1, -1):
@@ -360,7 +363,8 @@
 def scatter_rows(ids, table, gain, collective_id):
     n_dev = N_Z * N_Y * 2
     vocab, width = table.shape
-    n_chunks, _, n_tok = ids.shape
+    n_chunks = N_CHUNKS
+    n_tok = ids.shape[1] // n_chunks
     rows = n_tok // n_dev
     vocab_pad = -(-vocab // 256) * 256
     out = jax.ShapeDtypeStruct((n_chunks * rows, width), jnp.bfloat16)
@@ -375,11 +379,12 @@
             pltpu.VMEM((n_tok, vocab_pad), jnp.bfloat16),
             pltpu.VMEM((n_chunks, n_tok, width), jnp.bfloat16),
             pltpu.VMEM((rows, width), jnp.float32),
+            pltpu.VMEM((n_dev, rows * n_chunks, 128), jnp.int32),
             pltpu.SemaphoreType.DMA,
         ] + chunk_bufs(n_chunks, rows, width) + chunk_sems(Scatter, n_chunks),
         compiler_params=pltpu.CompilerParams(collective_id=collective_id, has_side_effects=True, vmem_limit_bytes=VMEM_LIMIT),
         name="scatter_rows",
-    )(ids, gain.reshape(1, width), table)
+    )(ids, gain, table)
 
 
 KEY_BLOCK = 512
@@ -401,6 +406,7 @@
     full[me] = own_ref[...]
     for pos, w_ref in enumerate((wq_ref, wk_ref, wv_ref)):
         w_all[:, pos * dim:(pos + 1) * dim] = w_ref[...]
+    columns = [jnp.broadcast_to(ref[...].astype(jnp.float32).reshape(1, -1), (dim, dim)).T[:, :1] for ref in (qg_ref, kg_ref)]
     packed = jnp.where(z == 0, 228, jnp.where(z == 1, 225, jnp.where(z == 2, 30, 27)))
 
     def event(e, carry):
@@ -478,8 +484,8 @@
         lanes = pl.ds(pl.multiple_of(blk * KEY_BLOCK, KEY_BLOCK), KEY_BLOCK)
         cos_b, sin_b = cos_ref[:, lanes], sin_ref[:, lanes]
         heads = []
-        for row, raw, gain in ((0, q_t, qg_ref), (1, k_t, kg_ref)):
-            normed = raw[:, lanes] * slots[0, row:row + 1, lanes] * gain[...]
+        for row, raw, gain in ((0, q_t, columns[0]), (1, k_t, columns[1])):
+            normed = raw[:, lanes] * slots[0, row:row + 1, lanes] * gain
             first, second = normed[:half], normed[half:]
             heads.append(jnp.concatenate([first * cos_b - second * sin_b, second * cos_b + first * sin_b], axis=0))
         q_b[:, lanes] = heads[0].astype(jnp.bfloat16)
@@ -558,7 +564,7 @@
 SUM_STEPS = {0: 0, 1: 1, 3: 2, 4: 3, 5: 4, 6: 5}
 
 
-def moe_kernel(n_chunks, exp_step, ctx_ref, wo_ref, x_ref, gain_ref, mask_ref, wr_ref, wg_ref, wu_ref, wd_ref, out_ref, acc_ref, gate_ref, full, part, total, m_own, h_own, *rest):
+def moe_kernel(n_chunks, exp_step, ctx_ref, wo_ref, x_ref, gain_ref, route_ref, wr_ref, wg_ref, wu_ref, wd_ref, out_ref, acc_ref, gate_ref, full, part, total, m_own, h_own, chosen, *rest):
     bufs, rest = rest[:6], rest[6:]
     n_sc = len(Scatter.SEMS)
     attn_sems, moe_sems, gather_sems = rest[:n_sc], rest[n_sc:2 * n_sc], rest[2 * n_sc:]
@@ -585,7 +591,7 @@
             attn_out = total[...].astype(jnp.bfloat16).astype(jnp.float32)
             hidden = (x_ref[loc_rows(k), :].astype(jnp.float32) + attn_out).astype(jnp.bfloat16)
             h_own[loc_rows(k), :] = hidden
-            normed = norm_rows(hidden.astype(jnp.float32), gain_ref[...].astype(jnp.float32))
+            normed = norm_rows(hidden.astype(jnp.float32), gain_ref[...].astype(jnp.float32).reshape(1, -1))
             m_own[loc_rows(k), :] = normed
             full[k, pl.ds(pl.multiple_of(place.me * rows, rows), rows), :] = normed
 
@@ -602,10 +608,23 @@
             project(k)
             attn_stage(0, k)
         attn_stage(1, 0)
-        for k in range(2, n_chunks):
+
+        def project_next(k, carry):
             project(k)
             attn_stage(0, k)
+            return carry
+
+        lax.fori_loop(2, n_chunks, project_next, 0)
         attn_stage(1, 1)
+        for dev in range(n_tok // rows):
+            routes = route_ref[:, dev * rows * n_chunks:(dev + 1) * rows * n_chunks]
+            expert = lax.broadcasted_iota(jnp.int32, (n_exp, rows * n_chunks), 0)
+            hits = jnp.zeros(expert.shape, jnp.float32)
+            for choice in range(routes.shape[0]):
+                hits = jnp.where(routes[choice:choice + 1] == expert, 1.0, hits)
+            picked = jnp.concatenate([hits, jnp.zeros_like(hits)], axis=0).T
+            for k in range(n_chunks):
+                chosen[k, dev * rows:(dev + 1) * rows, :] = picked[k * rows:(k + 1) * rows, :n_exp]
         for number in range(2, N_STAGES):
             attn_stage(number, 0)
         attn_stage(2, 1)
@@ -635,10 +654,15 @@
                 def _():
                     attn_stage(SUM_STEPS[at], 2)
 
-    for at_chunk, at, number in ((0, 5, 1), (0, 7, 2), (1, 0, 3), (1, 1, 4), (1, 2, 5)):
-        @pl.when((step == at) & (chunk == at_chunk))
-        def _():
-            attn_stage(number, 3)
+    for at, number in ((5, 1), (7, 2)):
+        @pl.when((step == at) & (chunk + 3 < n_chunks))
+        def _():
+            attn_stage(number, chunk + 3)
+
+    for at, number in ((0, 3), (1, 4), (2, 5)):
+        @pl.when((step == at) & (chunk > 0) & (chunk + 2 < n_chunks))
+        def _():
+            attn_stage(number, chunk + 2)
 
     @pl.when((step == 0) & (chunk > 0))
     def _():
@@ -649,7 +673,7 @@
         logits = lax.dot_general(full[chunk], wr_ref[...], nt_dims, preferred_element_type=jnp.float32)
         logits = logits - jnp.max(logits, axis=-1, keepdims=True)
         expd = jnp.exp(logits)
-        gates = expd / jnp.sum(expd, axis=-1, keepdims=True) * mask_ref[0]
+        gates = expd / jnp.sum(expd, axis=-1, keepdims=True) * chosen[chunk]
         for grp in range(n_exp // exp_step):
             gate_ref[grp] = gates[:, grp * exp_step:(grp + 1) * exp_step]
         acc_ref[...] = jnp.zeros_like(acc_ref)
@@ -690,9 +714,10 @@
         lax.fori_loop(0, n_chunks, drain, 0)
 
 
-def moe_layer(ctx, w_out, x_loc, gain, mask, wr_t, wg_t, wu_t, w_dn, collective_id):
+def moe_layer(ctx, w_out, x_loc, gain, routes, wr_t, wg_t, wu_t, w_dn, collective_id):
     rows_loc, width = x_loc.shape
-    n_chunks, n_tok, n_exp = mask.shape
+    n_chunks, n_tok = ctx.shape[:2]
+    n_exp = wr_t.shape[0]
     n_ff = wg_t.shape[0]
     step_cols = n_ff // n_exp * EXP_PER_STEP
     rows = rows_loc // n_chunks
@@ -704,8 +729,8 @@
             pl.BlockSpec(ctx.shape, lambda k, s: (0, 0, 0)),
             pl.BlockSpec(w_out.shape, const),
             pl.BlockSpec((rows_loc, width), const),
-            pl.BlockSpec((1, width), const),
-            pl.BlockSpec((1, n_tok, n_exp), lambda k, s: (k, 0, 0)),
+            pl.BlockSpec((width,), lambda k, s: (0,)),
+            pl.BlockSpec(routes.shape, const),
             pl.BlockSpec((n_exp, width), const),
             pl.BlockSpec((step_cols, width), lambda k, s: (s, 0)),
             pl.BlockSpec((step_cols, width), lambda k, s: (s, 0)),
@@ -721,10 +746,11 @@
             pltpu.VMEM((rows, width), jnp.float32),
             pltpu.VMEM((rows_loc, width), jnp.bfloat16),
             pltpu.VMEM((rows_loc, width), jnp.bfloat16),
+            pltpu.VMEM((n_chunks, n_tok, n_exp), jnp.float32),
         ] + chunk_bufs(n_chunks, rows, width) + chunk_sems(Scatter, n_chunks) + chunk_sems(Scatter, n_chunks) + chunk_sems(Gather, n_chunks),
         compiler_params=pltpu.CompilerParams(dimension_semantics=("arbitrary", "arbitrary"), collective_id=collective_id, has_side_effects=True, vmem_limit_bytes=VMEM_LIMIT),
         name="moe_layer",
-    )(ctx, w_out, x_loc, gain.reshape(1, width), mask, wr_t, wg_t, wu_t, w_dn)
+    )(ctx, w_out, x_loc, gain, routes, wr_t, wg_t, wu_t, w_dn)
 
 
 def solution(mesh):
@@ -734,22 +760,15 @@
     def device_fn(token_ids, route_idx, embed_table, attn_norm, w_query, w_key, w_value, w_out, q_gain, k_gain, mlp_norm, w_router, w_gate, w_up, w_down):
         batch_loc, seq_len = token_ids.shape
         model_dim = embed_table.shape[1]
-        ids = token_ids.reshape(tp_size, N_CHUNKS, -1).swapaxes(0, 1).reshape(N_CHUNKS, 1, -1)
-        x_loc, a_loc = scatter_rows(ids, embed_table, attn_norm, 0)
+        x_loc, a_loc = scatter_rows(token_ids.reshape(1, -1), embed_table, attn_norm, 0)
         cos_t, sin_t = (jnp.asarray(tab) for tab in rope_tables(seq_len))
-        as_column = lambda gain: gain.astype(jnp.float32).reshape(-1, 1)
-        context = attend_rows(a_loc, w_query, w_key, w_value, as_column(q_gain), as_column(k_gain), cos_t, sin_t, 1)
-        n_exp = w_gate.shape[0]
+        context = attend_rows(a_loc, w_query, w_key, w_value, q_gain, k_gain, cos_t, sin_t, 1)
         wg_t = jnp.swapaxes(w_gate, 1, 2).reshape(-1, model_dim)
         wu_t = jnp.swapaxes(w_up, 1, 2).reshape(-1, model_dim)
         w_dn = w_down.reshape(-1, model_dim)
         wr_t = w_router.T
-        expert_iota = jnp.arange(n_exp, dtype=jnp.int32)
-        chosen = route_idx.reshape(batch_loc * seq_len, -1)
-        mask = jnp.any(chosen[:, :, None] == expert_iota[None, None, :], axis=1).astype(jnp.float32)
-        rows_chunk = x_loc.shape[0] // N_CHUNKS
-        to_chunks = lambda arr: arr.reshape(tp_size, N_CHUNKS, rows_chunk, -1).swapaxes(0, 1).reshape(N_CHUNKS, tp_size * rows_chunk, -1)
-        out_loc = moe_layer(context, w_out, x_loc, mlp_norm, to_chunks(mask), wr_t, wg_t, wu_t, w_dn, 4)
+        routes = jnp.swapaxes(route_idx, 1, 2).reshape(route_idx.shape[-1], -1)
+        out_loc = moe_layer(context, w_out, x_loc, mlp_norm, routes, wr_t, wg_t, wu_t, w_dn, 4)
         return out_loc.reshape(batch_loc, -1, model_dim)
 
     return jax.shard_map(device_fn, mesh=mesh, in_specs=in_specs, out_specs=P("dp", "tp", None), check_vma=False)

time: 421 us -> 435 us (1.033)
  Pallas kernels: 408 us -> 433 us
  local copies, waits for them, and re-layouts: 8.61 us -> 1.88 us
    pallas_call x1, Pallas kernels: 254 us -> 279 us  [moe_layer(): pl.pallas_call(functools.partial(moe_kernel, n_chunks, EXP_PER_STEP), gri...]
    reshape x9 -> x0, local copies, waits for them, and re-layouts: 6.22 us -> none  [the longest x2 1.46 us: device_fn(): as_column = lambda gain: gain.astype(jnp.float32).reshape(-1, 1)]
where the time goes in v2:
time: 435 us
  Pallas kernels  433 us (100%)
    pallas_call x1, Pallas kernels, moe_layer(): pl.pallas_call(functools.partial(moe_kernel, n_chunks, EXP_PER_STEP), gri...  279 us
    pallas_call x1, Pallas kernels, scatter_rows(): pl.pallas_call(functools.partial(scatter_kernel, n_chunks), in_specs=[vme...  82.3 us
    pallas_call x1, Pallas kernels, attend_rows(): pl.pallas_call(attend_kernel, in_specs=[pl.BlockSpec(memory_space=pltpu.V...  72.3 us

profile of v2, /device:TPU:0, one launch (start us, length us, event | category | flops | bytes accessed | tf_op | source)
XLA Modules:
  0.0 435.1 jit_solution(14959015159489666420)
XLA Ops:
  0.0 82.3 %scatter_rows.1 = (bf16[128,2048]{1,0:T(8,128)(2,1)}, bf16[128,2048]{1,0:T(8,128)(2,1)}) custom-call(s32[1,2048]{1,0:T(1,128)} %ids_ref.1, bf16[2048]{0:T(1024)(128)(2,1)} %gain.1, bf16[3144,2048]{1,0:T(8,128)(2,1)} %table_ref.1), custom_call_target="tpu_custom_call" | custom-call | tf_op jit(solution)/shard_map/scatter_rows/pallas_call | solution.py:372
  82.3 72.3 %attend_rows.1.ctx_ref = bf16[8,256,128]{2,1,0:T(8,128)(2,1)} custom-call(bf16[128,2048]{1,0:T(8,128)(2,1)} %get-tuple-element.7.own_ref, bf16[2048,128]{1,0:T(8,128)(2,1)} %wq_ref.1, bf16[2048,128]{1,0:T(8,128)(2,1)} %wk_ref.1, bf16[2048,128]{1,0:T(8,128)(2,1)} %wv_ref.1, bf16[128]{0:T(256)(128)(2,1)} %qg_ref.1, bf16[128]{0:T(256)(128)(2,1)} %kg_ref.1, ...), custom_call_target="tpu_custom_call" | custom-call | tf_op jit(solution)/shard_map/attend_rows/pallas_call | solution.py:540
  154.6 278.6 %moe_layer.1 = bf16[128,2048]{1,0:T(8,128)(2,1)} custom-call(bf16[8,256,128]{2,1,0:T(8,128)(2,1)} %attend_rows.1.ctx_ref, bf16[128,2048]{1,0:T(8,128)(2,1)} %wo_ref.1, bf16[128,2048]{1,0:T(8,128)(2,1)} %get-tuple-element.8.x_ref, bf16[2048]{0:T(1024)(128)(2,1)} %gain_ref.1, s32[8,2048]{1,0:T(8,128)} %bitcast.17, bf16[64,2048]{1,0:T(8,128)(2,1)} %bitcast.16, ...), custom_call_target="tpu_custom_call" | custom-call | tf_op jit(solution)/shard_map/moe_layer/pallas_call | solution.py:725
  433.2 1.9 copy.19

commit v3 on v2

--- a/solution.py
+++ b/solution.py
@@ -10,7 +10,8 @@
 
 HEAD_DIM = 128
 NORM_EPS = 1e-5
-N_CHUNKS = 8
+N_CHUNKS = 4
+N_TABLE_CHUNKS = 4
 EXP_PER_STEP = 8
 VMEM_LIMIT = 63 * 1024 * 1024
 
@@ -363,7 +364,7 @@
 def scatter_rows(ids, table, gain, collective_id):
     n_dev = N_Z * N_Y * 2
     vocab, width = table.shape
-    n_chunks = N_CHUNKS
+    n_chunks = N_TABLE_CHUNKS
     n_tok = ids.shape[1] // n_chunks
     rows = n_tok // n_dev
     vocab_pad = -(-vocab // 256) * 256

time: 435 us -> 410 us (0.943)
  Pallas kernels: 433 us -> 407 us
    pallas_call x1, Pallas kernels: 279 us -> 253 us  [moe_layer(): pl.pallas_call(functools.partial(moe_kernel, n_chunks, EXP_PER_STEP), gri...]
where the time goes in v3:
time: 410 us; the launch traced here: 409 us
  Pallas kernels  407 us (99%)
    pallas_call x1, Pallas kernels, moe_layer(): pl.pallas_call(functools.partial(moe_kernel, n_chunks, EXP_PER_STEP), gri...  253 us
    pallas_call x1, Pallas kernels, scatter_rows(): pl.pallas_call(functools.partial(scatter_kernel, n_chunks), in_specs=[vme...  80.9 us
    pallas_call x1, Pallas kernels, attend_rows(): pl.pallas_call(attend_kernel, in_specs=[pl.BlockSpec(memory_space=pltpu.V...  73.3 us

profile of v3, /device:TPU:0, one launch (start us, length us, event | category | flops | bytes accessed | tf_op | source)
XLA Modules:
  0.0 409.3 jit_solution(9832205697892270198)
XLA Ops:
  0.0 80.9 %scatter_rows.1 = (bf16[128,2048]{1,0:T(8,128)(2,1)}, bf16[128,2048]{1,0:T(8,128)(2,1)}) custom-call(s32[1,2048]{1,0:T(1,128)} %ids_ref.1, bf16[2048]{0:T(1024)(128)(2,1)} %gain.1, bf16[3144,2048]{1,0:T(8,128)(2,1)} %table_ref.1), custom_call_target="tpu_custom_call" | custom-call | tf_op jit(solution)/shard_map/scatter_rows/pallas_call | solution.py:373
  81.0 73.3 %attend_rows.1.ctx_ref = bf16[4,512,128]{2,1,0:T(8,128)(2,1)} custom-call(bf16[128,2048]{1,0:T(8,128)(2,1)} %get-tuple-element.7.own_ref, bf16[2048,128]{1,0:T(8,128)(2,1)} %wq_ref.1, bf16[2048,128]{1,0:T(8,128)(2,1)} %wk_ref.1, bf16[2048,128]{1,0:T(8,128)(2,1)} %wv_ref.1, bf16[128]{0:T(256)(128)(2,1)} %qg_ref.1, bf16[128]{0:T(256)(128)(2,1)} %kg_ref.1, ...), custom_call_target="tpu_custom_call" | custom-call | tf_op jit(solution)/shard_map/attend_rows/pallas_call | solution.py:541
  154.2 253.2 %moe_layer.1 = bf16[128,2048]{1,0:T(8,128)(2,1)} custom-call(bf16[4,512,128]{2,1,0:T(8,128)(2,1)} %attend_rows.1.ctx_ref, bf16[128,2048]{1,0:T(8,128)(2,1)} %wo_ref.1, bf16[128,2048]{1,0:T(8,128)(2,1)} %get-tuple-element.8.x_ref, bf16[2048]{0:T(1024)(128)(2,1)} %gain_ref.1, s32[8,2048]{1,0:T(8,128)} %bitcast.17, bf16[64,2048]{1,0:T(8,128)(2,1)} %bitcast.16, ...), custom_call_target="tpu_custom_call" | custom-call | tf_op jit(solution)/shard_map/moe_layer/pallas_call | solution.py:726
  407.4 1.9 copy.19
